TPU v7x, 32 devices: a whole 2x2x4 slice. The times are simulated.
32 devices in a mesh: mkt: 4 (over z), draw: 4 (over y, core), nest: 2 (over x).
Axes of the slice: x: 2, y: 2, z: 4, core: 2. Of those that a mesh axis runs over, the one named last changes fastest.
Arguments:
- features: bfloat16 [32, 512, 128], P(None, 'mkt'), may hold values from -1.5 to 1.5
- taste_draws: bfloat16 [128, 32, 512], P('mkt', None, 'draw'), may hold values from -4 to 4
- taste_scale: float32 [32], replicated, may hold values from 0.2 to 1
- nest_param: float32 [16], P('nest'), may hold values from 0.3 to 0.95
- members: int32 [16, 48], P('nest'), may hold values from -1 to 511, as said below
- log_share: float32 [512, 128], P('mkt'), may hold values from -10 to -7
Outputs:
- mean_utility: float32 [128, 768], P('mkt', 'nest')
- model_share: float32 [128, 768], P('mkt', 'nest')
Inputs may be any that keep to these rules, and one draw needn't show every extreme that they name: `members`: every product id 0 to 511 stands in exactly one slot; in each nest's row the ids fill the first slots and -1 fills the rest; each nest holds at least 16 products, and some nest fills all 48 slots.
All inputs are finite; a program needn't handle non-finite values.
Results may differ from a plain program's by a relative error of at most 0.0013.
The roundings to bfloat16 on the way count: a program that leaves them out, or rounds other values in their place, can miss the bound.
Values may be sent and summed in bfloat16 or wider, within the bound.
A program may use at most 64 MiB of HBM per device.

v0:
```python
import jax
import jax.numpy as jnp
from jax import lax
from jax.sharding import PartitionSpec as P

ITERS = 3


def revise(value_slot, slot_share, target, nest_rate, occupied):
    safe_share = jnp.where(occupied[None, :], slot_share, 1.0)
    moved_value = value_slot + (1.0 - nest_rate)[None, :] * (target - jnp.log(safe_share))
    return jnp.where(occupied[None, :], moved_value, 0.0)


def shards(features, taste_draws, taste_scale, nest_param, members, log_share):
    market_x = lax.all_to_all(features, "mkt", split_axis=2, concat_axis=1, tiled=True)
    market_log = lax.all_to_all(log_share, "mkt", split_axis=1, concat_axis=0, tiled=True)
    market_list = market_log.shape[1]
    product_count = market_log.shape[0]
    nest_count = members.shape[0]
    slot_count = members.shape[1]
    columns = nest_count * slot_count
    draws_here = taste_draws.shape[2]
    total_draws = draws_here * lax.axis_size("draw")
    product_ids = members.reshape(columns)
    occupied = product_ids >= 0
    safe_ids = jnp.maximum(product_ids, 0)
    live_flag = occupied.astype(jnp.float32)
    product_range = jnp.arange(product_count, dtype=jnp.int32)
    onehot = ((safe_ids[None, :] == product_range[:, None]) & occupied[None, :]).astype(
        jnp.bfloat16
    )
    slot_features = jnp.einsum(
        "kjm,js->mks", market_x, onehot, preferred_element_type=jnp.float32
    ).astype(jnp.bfloat16)
    slot_log = jnp.transpose(jnp.take(market_log, safe_ids, axis=0), (1, 0))
    outside = 1.0 - jnp.sum(jnp.exp(market_log), axis=0)
    value_slot = jnp.where(occupied[None, :], slot_log - jnp.log(outside)[:, None], 0.0)
    taste_matrix = (taste_scale[None, :, None] * taste_draws.astype(jnp.float32)).astype(
        jnp.bfloat16
    )
    nest_rate = jnp.repeat(nest_param, slot_count)
    mean_utility_part = jnp.einsum(
        "dve,dvb->deb", slot_features, taste_matrix, preferred_element_type=jnp.float32
    )
    slot_share = jnp.zeros_like(value_slot)
    for iteration in range(ITERS):
        utility = live_flag[None, :, None] * jnp.exp(
            (value_slot[:, :, None] + mean_utility_part) / nest_rate[None, :, None]
        )
        grouped = utility.reshape(market_list, nest_count, slot_count, draws_here)
        inner_sum = jnp.sum(grouped, axis=2)
        inclusive_value = jnp.exp(nest_param[None, :, None] * jnp.log(inner_sum))
        totals = lax.psum(jnp.sum(inclusive_value, axis=1), "nest")
        nest_ratio = inclusive_value / (inner_sum * (1.0 + totals)[:, None, :])
        share_terms = jnp.sum(grouped * nest_ratio[:, :, None, :], axis=3).reshape(
            market_list, columns
        )
        slot_share = lax.psum(share_terms, "draw") / total_draws
        value_slot = revise(value_slot, slot_share, slot_log, nest_rate, occupied)
    return (value_slot, slot_share)


def solution(mesh):
    in_specs = (
        P(None, "mkt", None),
        P("mkt", None, "draw"),
        P(),
        P("nest"),
        P("nest", None),
        P("mkt", None),
    )
    out_specs = (P("mkt", "nest"), P("mkt", "nest"))
    return jax.shard_map(shards, mesh=mesh, in_specs=in_specs, out_specs=out_specs, check_vma=False)
```

profile of v0, /device:TPU:1, one launch (start us, length us, event | category | flops | bytes accessed | tf_op | source)
XLA Modules:
  0.0 170.8 jit_solution(5884183083681372627)
XLA Ops:
  0.6 0.0 copy-start.1
  0.6 0.0 copy-start.2
  0.7 1.6 copy.23
  2.2 5.4 %all-to-all-start = ((f32[128,4,32]{0,2,1:T(8,128)}), f32[128,4,32]{0,2,1:T(8,128)S(1)}, u32[]{:S(2)}, u32[]{:S(2)}) async-start(f32[128,4,32]{0,2,1:T(8,128)} %bitcast), calls=%async_computation | async-start | bytes 131072 | tf_op jit(solution)/shard_map/all_to_all | solution.py:17
  7.7 0.7 broadcast_in_dim.85
  8.4 0.1 reshape.109
  8.5 2.7 %copy.26 = bf16[32,128,128]{1,0,2:T(8,128)(2,1)} copy(bf16[32,128,128]{2,1,0:T(8,128)(2,1)} %param.6) | data formatting | bytes 2097152 | tf_op args[0]
  11.2 1.1 all-to-all-done
  12.3 3.5 %all-to-all-start.1 = ((bf16[32,128,128]{1,0,2:T(8,128)(2,1)}), bf16[32,128,128]{1,0,2:T(8,128)(2,1)S(1)}, u32[]{:S(2)}, u32[]{:S(2)}) async-start(bf16[32,128,128]{1,0,2:T(8,128)(2,1)} %copy.26), calls=%async_computation.1 | async-start | bytes 2097152 | tf_op jit(solution)/shard_map/all_to_all | solution.py:16
  15.8 0.7 broadcast_maximum_fusion
  16.5 0.1 max.23
  16.5 0.7 broadcast_compare_fusion
  17.2 0.1 ge.22
  17.4 0.1 copy.24
  17.5 1.1 gather_fusion
  18.6 0.1 exponential_reduce_fusion
  18.8 0.2 fusion.15
  19.0 0.1 copy.25
  19.1 22.0 %all-to-all-done.1 = bf16[32,128,128]{1,0,2:T(8,128)(2,1)S(1)} async-done(((bf16[32,128,128]{1,0,2:T(8,128)(2,1)}), bf16[32,128,128]{1,0,2:T(8,128)(2,1)S(1)}, u32[]{:S(2)}, u32[]{:S(2)}) %all-to-all-start.1) | async-done | bytes 1048608 | tf_op jit(solution)/shard_map/all_to_all | solution.py:16
  41.0 0.0 copy-done.1
  41.0 0.0 copy-done.2
  41.0 6.5 %exponential_multiply_fusion.2 = (f32[32,384,128]{2,1,0:T(8,128)}, f32[32,384,128]{2,1,0:T(8,128)}) fusion(f32[384]{0:T(512)S(1)} %reshape.109, f32[32,384]{1,0:T(8,128)S(1)} %copy.25, f32[384]{0:T(512)S(1)} %convert_element_type.20, bf16[32,32,128]{2,1,0:T(8,128)(2,1)S(1)} %copy-done.1, f32[32]{0:T(128)S(1)} %copy-done.2, ...), kind=kOutput, calls=%fused_computation.6 | convolution fusion | flops 509214720 | bytes 13947904 | tf_op jit(solution)/shard_map/dve,dvb->deb/dot_general | solution.py:43
  47.5 0.0 copy-start
  47.5 3.7 %reduce_sum.91 = f32[32,8,128]{2,1,0:T(8,128)S(1)} reduce(f32[32,8,48,128]{3,2,1,0:T(8,128)} %bitcast.62, f32[]{:T(128)} %constant.28.clone.1), dimensions={2}, to_apply=%region_1.2 | reduce | flops 1540096 | bytes 6422532 | tf_op jit(solution)/shard_map/reduce_sum | solution.py:52
  51.2 0.0 copy-done
  51.2 0.1 fusion.27
  51.3 6.1 %psum.42 = f32[32,128]{1,0:T(8,128)S(1)} all-reduce(f32[32,128]{1,0:T(8,128)S(1)} %fusion.27), channel_id=1, replica_groups=mesh['mkt'=4,'draw'=4,'nest'=2] {'nest'}, use_global_device_ids=true, to_apply=%region_3.4 | all-reduce | flops 4096 | bytes 32768 | tf_op jit(solution)/shard_map/psum | solution.py:54
  57.4 0.1 multiply_divide_fusion.2
  57.5 6.2 %bitcast_multiply_fusion.2 = f32[32,384,128]{2,1,0:T(8,128)} fusion(f32[32,384,128]{2,1,0:T(8,128)} %get-tuple-element.10, f32[32,8,128]{2,1,0:T(8,128)S(1)} %multiply_divide_fusion.2), kind=kLoop, calls=%fused_computation.3 | loop fusion | flops 1572864 | bytes 12713984 | tf_op jit(solution)/shard_map/mul | solution.py:56
  63.8 4.5 %reduce_sum.93 = f32[32,384]{1,0:T(8,128)S(1)} reduce(f32[32,384,128]{2,1,0:T(8,128)} %bitcast_multiply_fusion.2, f32[]{:T(128)} %constant.28.clone.1), dimensions={2}, to_apply=%region_4.5 | reduce | flops 1560576 | bytes 6340612 | tf_op jit(solution)/shard_map/reduce_sum | solution.py:56
  68.2 0.1 copy.30
  68.4 15.4 %psum.43 = f32[32,384]{0,1:T(8,128)S(1)} all-reduce(f32[32,384]{0,1:T(8,128)S(1)} %copy.30), channel_id=1, replica_groups=mesh['mkt'=4,'draw'=4,'nest'=2] {'draw'}, use_global_device_ids=true, to_apply=%region_5.6 | all-reduce | flops 12288 | bytes 98304 | tf_op jit(solution)/shard_map/psum | solution.py:59
  83.7 0.2 fusion.18
  84.0 0.1 copy.31
  84.1 6.8 %exponential_multiply_fusion.1 = f32[32,384,128]{2,1,0:T(8,128)} fusion(f32[32,384,128]{2,1,0:T(8,128)} %get-tuple-element.11, f32[32,384]{1,0:T(8,128)S(1)} %copy.31, f32[384]{0:T(512)S(1)} %reshape.109, f32[384]{0:T(512)S(1)} %convert_element_type.20), kind=kLoop, calls=%fused_computation.5 | loop fusion | flops 4718592 | bytes 12635136 | tf_op jit(solution)/shard_map/mul | solution.py:48
  90.9 3.7 %reduce_sum.94 = f32[32,8,128]{2,1,0:T(8,128)S(1)} reduce(f32[32,8,48,128]{3,2,1,0:T(8,128)} %bitcast.63, f32[]{:T(128)} %constant.28.clone.1), dimensions={2}, to_apply=%region_6.7 | reduce | flops 1540096 | bytes 6422532 | tf_op jit(solution)/shard_map/reduce_sum | solution.py:52
  94.5 0.1 fusion.26
  94.6 5.2 %psum.44 = f32[32,128]{1,0:T(8,128)S(1)} all-reduce(f32[32,128]{1,0:T(8,128)S(1)} %fusion.26), channel_id=1, replica_groups=mesh['mkt'=4,'draw'=4,'nest'=2] {'nest'}, use_global_device_ids=true, to_apply=%region_8.9 | all-reduce | flops 4096 | bytes 32768 | tf_op jit(solution)/shard_map/psum | solution.py:54
  99.8 0.1 multiply_divide_fusion.1
  99.9 6.9 %bitcast_multiply_fusion.1 = f32[32,384,128]{2,1,0:T(8,128)} fusion(f32[32,8,128]{2,1,0:T(8,128)S(1)} %multiply_divide_fusion.1, f32[384]{0:T(512)S(1)} %reshape.109, f32[32,384,128]{2,1,0:T(8,128)} %get-tuple-element.11, f32[32,384]{1,0:T(8,128)S(1)} %copy.31, f32[384]{0:T(512)S(1)} %convert_element_type.20), kind=kLoop, calls=%fused_computation.2 | loop fusion | flops 6291456 | bytes 12766208 | tf_op jit(solution)/shard_map/mul | solution.py:56
  106.9 4.5 %reduce_sum.96 = f32[32,384]{1,0:T(8,128)S(1)} reduce(f32[32,384,128]{2,1,0:T(8,128)} %bitcast_multiply_fusion.1, f32[]{:T(128)} %constant.28.clone.1), dimensions={2}, to_apply=%region_9.10 | reduce | flops 1560576 | bytes 6340612 | tf_op jit(solution)/shard_map/reduce_sum | solution.py:56
  111.3 0.1 copy.32
  111.5 14.6 %psum.45 = f32[32,384]{0,1:T(8,128)S(1)} all-reduce(f32[32,384]{0,1:T(8,128)S(1)} %copy.32), channel_id=1, replica_groups=mesh['mkt'=4,'draw'=4,'nest'=2] {'draw'}, use_global_device_ids=true, to_apply=%region_10.11 | all-reduce | flops 12288 | bytes 98304 | tf_op jit(solution)/shard_map/psum | solution.py:59
  126.1 0.2 fusion.21
  126.3 0.1 copy.33
  126.4 6.8 %exponential_multiply_fusion = f32[32,384,128]{2,1,0:T(8,128)} fusion(f32[32,384,128]{2,1,0:T(8,128)} %get-tuple-element.11, f32[32,384]{1,0:T(8,128)S(1)} %copy.33, f32[384]{0:T(512)S(1)} %reshape.109, f32[384]{0:T(512)S(1)} %convert_element_type.20), kind=kLoop, calls=%fused_computation.4 | loop fusion | flops 4718592 | bytes 12635136 | tf_op jit(solution)/shard_map/mul | solution.py:48
  133.2 3.7 %reduce_sum.97 = f32[32,8,128]{2,1,0:T(8,128)S(1)} reduce(f32[32,8,48,128]{3,2,1,0:T(8,128)} %bitcast.64, f32[]{:T(128)} %constant.28.clone.1), dimensions={2}, to_apply=%region_11.12 | reduce | flops 1540096 | bytes 6422532 | tf_op jit(solution)/shard_map/reduce_sum | solution.py:52
  136.9 0.1 fusion.25
  137.0 6.1 %psum.46 = f32[32,128]{1,0:T(8,128)S(1)} all-reduce(f32[32,128]{1,0:T(8,128)S(1)} %fusion.25), channel_id=1, replica_groups=mesh['mkt'=4,'draw'=4,'nest'=2] {'nest'}, use_global_device_ids=true, to_apply=%region_13.14 | all-reduce | flops 4096 | bytes 32768 | tf_op jit(solution)/shard_map/psum | solution.py:54
  143.1 0.1 multiply_divide_fusion
  143.2 6.9 %bitcast_multiply_fusion = f32[32,384,128]{2,1,0:T(8,128)} fusion(f32[32,8,128]{2,1,0:T(8,128)S(1)} %multiply_divide_fusion, f32[384]{0:T(512)S(1)} %reshape.109, f32[32,384,128]{2,1,0:T(8,128)} %get-tuple-element.11, f32[32,384]{1,0:T(8,128)S(1)} %copy.33, f32[384]{0:T(512)S(1)} %convert_element_type.20), kind=kLoop, calls=%fused_computation.1 | loop fusion | flops 6291456 | bytes 12766208 | tf_op jit(solution)/shard_map/mul | solution.py:56
  150.1 4.5 %reduce_sum.99 = f32[32,384]{1,0:T(8,128)S(1)} reduce(f32[32,384,128]{2,1,0:T(8,128)} %bitcast_multiply_fusion, f32[]{:T(128)} %constant.28.clone.1), dimensions={2}, to_apply=%region_14.15 | reduce | flops 1560576 | bytes 6340612 | tf_op jit(solution)/shard_map/reduce_sum | solution.py:56
  154.6 0.1 copy.34
  154.7 14.4 %psum.47 = f32[32,384]{0,1:T(8,128)S(1)} all-reduce(f32[32,384]{0,1:T(8,128)S(1)} %copy.34), channel_id=1, replica_groups=mesh['mkt'=4,'draw'=4,'nest'=2] {'draw'}, use_global_device_ids=true, to_apply=%region_15.16 | all-reduce | flops 12288 | bytes 98304 | tf_op jit(solution)/shard_map/psum | solution.py:59
  169.1 0.2 broadcast_multiply_fusion
  169.4 0.7 copy.35
  170.1 0.7 copy.36
  (8 shorter events, 0.0 us)
Async XLA Ops:
  0.6 40.4 %copy-start.1 = (bf16[32,32,128]{2,1,0:T(8,128)(2,1)S(1)}, bf16[32,32,128]{2,1,0:T(8,128)(2,1)}, u32[]{:S(2)}) copy-start(bf16[32,32,128]{2,1,0:T(8,128)(2,1)} %param.7) | copy-start | bytes 786436
  0.6 40.4 %copy-start.2 = (f32[32]{0:T(128)S(1)}, f32[32]{0:T(128)}, u32[]{:S(2)}) copy-start(f32[32]{0:T(128)} %param.8) | copy-start | bytes 388
  2.2 10.0 %all-to-all-start = ((f32[128,4,32]{0,2,1:T(8,128)}), f32[128,4,32]{0,2,1:T(8,128)S(1)}, u32[]{:S(2)}, u32[]{:S(2)}) async-start(f32[128,4,32]{0,2,1:T(8,128)} %bitcast), calls=%async_computation | async-start | bytes 131072 | tf_op jit(solution)/shard_map/all_to_all | solution.py:17
  12.3 28.8 %all-to-all-start.1 = ((bf16[32,128,128]{1,0,2:T(8,128)(2,1)}), bf16[32,128,128]{1,0,2:T(8,128)(2,1)S(1)}, u32[]{:S(2)}, u32[]{:S(2)}) async-start(bf16[32,128,128]{1,0,2:T(8,128)(2,1)} %copy.26), calls=%async_computation.1 | async-start | bytes 2097152 | tf_op jit(solution)/shard_map/all_to_all | solution.py:16
  47.5 3.7 %copy-start = (f32[8]{0:T(128)S(1)}, f32[8]{0:T(128)}, u32[]{:S(2)}) copy-start(f32[8]{0:T(128)} %param.9) | copy-start | bytes 100
where the time goes:
time: 172 us; the launch traced here: 171 us
  blocking collectives  61.8 us (36%)
  other arithmetic  61.1 us (36%)
  waiting for transfers between devices  23.1 us (13%)
  starting transfers between devices  8.92 us (5%)
  local copies, waits for them, and re-layouts  8.63 us (5%)
  matrix products  6.48 us (4%)
    psum x3, blocking collectives, shards(): slot_share = lax.psum(share_terms, 'draw') / total_draws  44.3 us
    all_to_all x1, waiting for transfers between devices, shards(): lax.all_to_all(features, 'mkt', split_axis=2, concat_axis=1, tiled=True)  22 us
    mul x3, other arithmetic, shards(): grouped * nest_ratio[:, :, None, :]  20.1 us
    psum x3, blocking collectives, shards(): totals = lax.psum(jnp.sum(inclusive_value, axis=1), 'nest')  17.4 us
    mul x2, other arithmetic, shards(): live_flag[None, :, None]  13.6 us
    reduce_sum x3, other arithmetic, shards(): jnp.sum(grouped * nest_ratio[:, :, None, :], axis=3)  13.4 us
    reduce_sum x3, other arithmetic, shards(): inner_sum = jnp.sum(grouped, axis=2)  11 us
    dot_general x1, matrix products, shards(): jnp.einsum('dve,dvb->deb', slot_features, taste_matrix, preferred_element...  6.48 us
  transfers between devices with their start and end apart: 2, of which 2 were waited for; matrix products, arithmetic and copies ran while one was open for 4% of the time, Pallas kernels for 0%

commit v1 on v0

--- a/solution.py
+++ b/solution.py
@@ -51,7 +51,7 @@
         grouped = utility.reshape(market_list, nest_count, slot_count, draws_here)
         inner_sum = jnp.sum(grouped, axis=2)
         inclusive_value = jnp.exp(nest_param[None, :, None] * jnp.log(inner_sum))
-        totals = lax.psum(jnp.sum(inclusive_value, axis=1), "nest")
+        totals = jnp.sum(lax.all_gather(jnp.sum(inclusive_value, axis=1), "nest"), axis=0)
         nest_ratio = inclusive_value / (inner_sum * (1.0 + totals)[:, None, :])
         share_terms = jnp.sum(grouped * nest_ratio[:, :, None, :], axis=3).reshape(
             market_list, columns

time: 172 us -> 161 us (0.936)
  blocking collectives: 61.8 us -> 51.5 us
    psum x3 -> x0, blocking collectives: 17.4 us -> none  [shards(): totals = lax.psum(jnp.sum(inclusive_value, axis=1), 'nest')]
    all_gather x0 -> x3, blocking collectives: none -> 9.76 us  [shards(): lax.all_gather(jnp.sum(inclusive_value, axis=1), 'nest')]
    psum x3, blocking collectives: 44.3 us -> 41.7 us  [shards(): slot_share = lax.psum(share_terms, 'draw') / total_draws]
where the time goes in v1:
time: 161 us
  other arithmetic  61.2 us (38%)
  blocking collectives  51.5 us (32%)
  waiting for transfers between devices  23.1 us (14%)
  starting transfers between devices  8.92 us (6%)
  local copies, waits for them, and re-layouts  8.63 us (5%)
  matrix products  6.48 us (4%)
    psum x3, blocking collectives, shards(): slot_share = lax.psum(share_terms, 'draw') / total_draws  41.7 us
    all_to_all x1, waiting for transfers between devices, shards(): lax.all_to_all(features, 'mkt', split_axis=2, concat_axis=1, tiled=True)  22 us
    mul x3, other arithmetic, shards(): grouped * nest_ratio[:, :, None, :]  20.1 us
    mul x2, other arithmetic, shards(): live_flag[None, :, None]  13.6 us
    reduce_sum x3, other arithmetic, shards(): jnp.sum(grouped * nest_ratio[:, :, None, :], axis=3)  13.4 us
    reduce_sum x3, other arithmetic, shards(): inner_sum = jnp.sum(grouped, axis=2)  11 us
    all_gather x3, blocking collectives, shards(): lax.all_gather(jnp.sum(inclusive_value, axis=1), 'nest')  9.76 us
    dot_general x1, matrix products, shards(): jnp.einsum('dve,dvb->deb', slot_features, taste_matrix, preferred_element...  6.48 us
  transfers between devices with their start and end apart: 2, of which 2 were waited for; matrix products, arithmetic and copies ran while one was open for 4% of the time, Pallas kernels for 0%

profile of v1, /device:TPU:1, one launch (start us, length us, event | category | flops | bytes accessed | tf_op | source)
XLA Modules:
  0.0 160.6 jit_solution(1288049078247704146)
XLA Ops:
  0.6 0.0 copy-start.1
  0.6 0.0 copy-start.2
  0.7 1.6 copy.37
  2.2 5.4 %all-to-all-start = ((f32[128,4,32]{0,2,1:T(8,128)}), f32[128,4,32]{0,2,1:T(8,128)S(1)}, u32[]{:S(2)}, u32[]{:S(2)}) async-start(f32[128,4,32]{0,2,1:T(8,128)} %bitcast), calls=%async_computation | async-start | bytes 131072 | tf_op jit(solution)/shard_map/all_to_all | solution.py:17
  7.7 0.7 broadcast_in_dim.85
  8.4 0.1 reshape.115
  8.5 2.7 %copy.40 = bf16[32,128,128]{1,0,2:T(8,128)(2,1)} copy(bf16[32,128,128]{2,1,0:T(8,128)(2,1)} %param.6) | data formatting | bytes 2097152 | tf_op args[0]
  11.2 1.1 all-to-all-done
  12.3 3.5 %all-to-all-start.1 = ((bf16[32,128,128]{1,0,2:T(8,128)(2,1)}), bf16[32,128,128]{1,0,2:T(8,128)(2,1)S(1)}, u32[]{:S(2)}, u32[]{:S(2)}) async-start(bf16[32,128,128]{1,0,2:T(8,128)(2,1)} %copy.40), calls=%async_computation.1 | async-start | bytes 2097152 | tf_op jit(solution)/shard_map/all_to_all | solution.py:16
  15.8 0.7 broadcast_maximum_fusion
  16.5 0.1 max.23
  16.5 0.7 broadcast_compare_fusion
  17.2 0.1 ge.22
  17.4 0.1 copy.38
  17.5 1.1 gather_fusion
  18.6 0.1 exponential_reduce_fusion
  18.8 0.2 fusion.15
  19.0 0.1 copy.39
  19.1 22.0 %all-to-all-done.1 = bf16[32,128,128]{1,0,2:T(8,128)(2,1)S(1)} async-done(((bf16[32,128,128]{1,0,2:T(8,128)(2,1)}), bf16[32,128,128]{1,0,2:T(8,128)(2,1)S(1)}, u32[]{:S(2)}, u32[]{:S(2)}) %all-to-all-start.1) | async-done | bytes 1048608 | tf_op jit(solution)/shard_map/all_to_all | solution.py:16
  41.0 0.0 copy-done.1
  41.0 0.0 copy-done.2
  41.0 6.5 %exponential_multiply_fusion.2 = (f32[32,384,128]{2,1,0:T(8,128)}, f32[32,384,128]{2,1,0:T(8,128)}) fusion(f32[384]{0:T(512)S(1)} %reshape.115, f32[32,384]{1,0:T(8,128)S(1)} %copy.39, f32[384]{0:T(512)S(1)} %convert_element_type.20, bf16[32,32,128]{2,1,0:T(8,128)(2,1)S(1)} %copy-done.1, f32[32]{0:T(128)S(1)} %copy-done.2, ...), kind=kOutput, calls=%fused_computation.6 | convolution fusion | flops 509214720 | bytes 13947904 | tf_op jit(solution)/shard_map/dve,dvb->deb/dot_general | solution.py:43
  47.5 0.0 copy-start
  47.5 3.7 %reduce_sum.118 = f32[32,8,128]{2,1,0:T(8,128)S(1)} reduce(f32[32,8,48,128]{3,2,1,0:T(8,128)} %bitcast.65, f32[]{:T(128)} %constant.28.clone.1), dimensions={2}, to_apply=%region_1.2 | reduce | flops 1540096 | bytes 6422532 | tf_op jit(solution)/shard_map/reduce_sum | solution.py:52
  51.2 0.0 copy-done
  51.2 0.1 fusion.27
  51.3 3.3 %all-gather = f32[64,128]{1,0:T(8,128)S(1)} all-gather(f32[32,128]{1,0:T(8,128)S(1)} %fusion.27), channel_id=2, replica_groups=mesh['mkt'=4,'draw'=4,'nest'=2] {'nest'}, dimensions={0}, use_global_device_ids=true | all-gather | bytes 49152 | tf_op jit(solution)/shard_map/all_gather | solution.py:54
  54.6 0.1 multiply_divide_fusion.2
  54.7 6.2 %bitcast_multiply_fusion.2 = f32[32,384,128]{2,1,0:T(8,128)} fusion(f32[32,384,128]{2,1,0:T(8,128)} %get-tuple-element.12, f32[32,8,128]{2,1,0:T(8,128)S(1)} %multiply_divide_fusion.2), kind=kLoop, calls=%fused_computation.3 | loop fusion | flops 1572864 | bytes 12713984 | tf_op jit(solution)/shard_map/mul | solution.py:56
  60.9 4.5 %reduce_sum.121 = f32[32,384]{1,0:T(8,128)S(1)} reduce(f32[32,384,128]{2,1,0:T(8,128)} %bitcast_multiply_fusion.2, f32[]{:T(128)} %constant.28.clone.1), dimensions={2}, to_apply=%region_4.5 | reduce | flops 1560576 | bytes 6340612 | tf_op jit(solution)/shard_map/reduce_sum | solution.py:56
  65.4 0.1 copy.44
  65.5 14.5 %psum.21 = f32[32,384]{0,1:T(8,128)S(1)} all-reduce(f32[32,384]{0,1:T(8,128)S(1)} %copy.44), channel_id=1, replica_groups=mesh['mkt'=4,'draw'=4,'nest'=2] {'draw'}, use_global_device_ids=true, to_apply=%region_5.6 | all-reduce | flops 12288 | bytes 98304 | tf_op jit(solution)/shard_map/psum | solution.py:59
  80.0 0.2 fusion.18
  80.2 0.1 copy.45
  80.3 6.8 %exponential_multiply_fusion.1 = f32[32,384,128]{2,1,0:T(8,128)} fusion(f32[32,384,128]{2,1,0:T(8,128)} %get-tuple-element.13, f32[32,384]{1,0:T(8,128)S(1)} %copy.45, f32[384]{0:T(512)S(1)} %reshape.115, f32[384]{0:T(512)S(1)} %convert_element_type.20), kind=kLoop, calls=%fused_computation.5 | loop fusion | flops 4718592 | bytes 12635136 | tf_op jit(solution)/shard_map/mul | solution.py:48
  87.1 3.7 %reduce_sum.122 = f32[32,8,128]{2,1,0:T(8,128)S(1)} reduce(f32[32,8,48,128]{3,2,1,0:T(8,128)} %bitcast.66, f32[]{:T(128)} %constant.28.clone.1), dimensions={2}, to_apply=%region_6.7 | reduce | flops 1540096 | bytes 6422532 | tf_op jit(solution)/shard_map/reduce_sum | solution.py:52
  90.8 0.1 fusion.26
  90.9 3.3 %all-gather.1 = f32[64,128]{1,0:T(8,128)S(1)} all-gather(f32[32,128]{1,0:T(8,128)S(1)} %fusion.26), channel_id=3, replica_groups=mesh['mkt'=4,'draw'=4,'nest'=2] {'nest'}, dimensions={0}, use_global_device_ids=true | all-gather | bytes 49152 | tf_op jit(solution)/shard_map/all_gather | solution.py:54
  94.2 0.1 multiply_divide_fusion.1
  94.3 6.9 %bitcast_multiply_fusion.1 = f32[32,384,128]{2,1,0:T(8,128)} fusion(f32[32,8,128]{2,1,0:T(8,128)S(1)} %multiply_divide_fusion.1, f32[384]{0:T(512)S(1)} %reshape.115, f32[32,384,128]{2,1,0:T(8,128)} %get-tuple-element.13, f32[32,384]{1,0:T(8,128)S(1)} %copy.45, f32[384]{0:T(512)S(1)} %convert_element_type.20), kind=kLoop, calls=%fused_computation.2 | loop fusion | flops 6291456 | bytes 12766208 | tf_op jit(solution)/shard_map/mul | solution.py:56
  101.2 4.5 %reduce_sum.125 = f32[32,384]{1,0:T(8,128)S(1)} reduce(f32[32,384,128]{2,1,0:T(8,128)} %bitcast_multiply_fusion.1, f32[]{:T(128)} %constant.28.clone.1), dimensions={2}, to_apply=%region_9.10 | reduce | flops 1560576 | bytes 6340612 | tf_op jit(solution)/shard_map/reduce_sum | solution.py:56
  105.7 0.1 copy.46
  105.8 13.7 %psum.22 = f32[32,384]{0,1:T(8,128)S(1)} all-reduce(f32[32,384]{0,1:T(8,128)S(1)} %copy.46), channel_id=1, replica_groups=mesh['mkt'=4,'draw'=4,'nest'=2] {'draw'}, use_global_device_ids=true, to_apply=%region_10.11 | all-reduce | flops 12288 | bytes 98304 | tf_op jit(solution)/shard_map/psum | solution.py:59
  119.5 0.2 fusion.21
  119.8 0.1 copy.47
  119.9 6.8 %exponential_multiply_fusion = f32[32,384,128]{2,1,0:T(8,128)} fusion(f32[32,384,128]{2,1,0:T(8,128)} %get-tuple-element.13, f32[32,384]{1,0:T(8,128)S(1)} %copy.47, f32[384]{0:T(512)S(1)} %reshape.115, f32[384]{0:T(512)S(1)} %convert_element_type.20), kind=kLoop, calls=%fused_computation.4 | loop fusion | flops 4718592 | bytes 12635136 | tf_op jit(solution)/shard_map/mul | solution.py:48
  126.7 3.7 %reduce_sum.126 = f32[32,8,128]{2,1,0:T(8,128)S(1)} reduce(f32[32,8,48,128]{3,2,1,0:T(8,128)} %bitcast.67, f32[]{:T(128)} %constant.28.clone.1), dimensions={2}, to_apply=%region_11.12 | reduce | flops 1540096 | bytes 6422532 | tf_op jit(solution)/shard_map/reduce_sum | solution.py:52
  130.3 0.1 fusion.25
  130.4 3.3 %all-gather.2 = f32[64,128]{1,0:T(8,128)S(1)} all-gather(f32[32,128]{1,0:T(8,128)S(1)} %fusion.25), channel_id=4, replica_groups=mesh['mkt'=4,'draw'=4,'nest'=2] {'nest'}, dimensions={0}, use_global_device_ids=true | all-gather | bytes 49152 | tf_op jit(solution)/shard_map/all_gather | solution.py:54
  133.7 0.1 multiply_divide_fusion
  133.8 6.9 %bitcast_multiply_fusion = f32[32,384,128]{2,1,0:T(8,128)} fusion(f32[32,8,128]{2,1,0:T(8,128)S(1)} %multiply_divide_fusion, f32[384]{0:T(512)S(1)} %reshape.115, f32[32,384,128]{2,1,0:T(8,128)} %get-tuple-element.13, f32[32,384]{1,0:T(8,128)S(1)} %copy.47, f32[384]{0:T(512)S(1)} %convert_element_type.20), kind=kLoop, calls=%fused_computation.1 | loop fusion | flops 6291456 | bytes 12766208 | tf_op jit(solution)/shard_map/mul | solution.py:56
  140.8 4.5 %reduce_sum.129 = f32[32,384]{1,0:T(8,128)S(1)} reduce(f32[32,384,128]{2,1,0:T(8,128)} %bitcast_multiply_fusion, f32[]{:T(128)} %constant.28.clone.1), dimensions={2}, to_apply=%region_14.15 | reduce | flops 1560576 | bytes 6340612 | tf_op jit(solution)/shard_map/reduce_sum | solution.py:56
  145.2 0.1 copy.48
  145.4 13.5 %psum.23 = f32[32,384]{0,1:T(8,128)S(1)} all-reduce(f32[32,384]{0,1:T(8,128)S(1)} %copy.48), channel_id=1, replica_groups=mesh['mkt'=4,'draw'=4,'nest'=2] {'draw'}, use_global_device_ids=true, to_apply=%region_15.16 | all-reduce | flops 12288 | bytes 98304 | tf_op jit(solution)/shard_map/psum | solution.py:59
  158.9 0.2 broadcast_multiply_fusion
  159.1 0.7 copy.49
  159.9 0.7 copy.50
  (11 shorter events, 0.1 us)
Async XLA Ops:
  0.6 40.4 %copy-start.1 = (bf16[32,32,128]{2,1,0:T(8,128)(2,1)S(1)}, bf16[32,32,128]{2,1,0:T(8,128)(2,1)}, u32[]{:S(2)}) copy-start(bf16[32,32,128]{2,1,0:T(8,128)(2,1)} %param.7) | copy-start | bytes 786436
  0.6 40.4 %copy-start.2 = (f32[32]{0:T(128)S(1)}, f32[32]{0:T(128)}, u32[]{:S(2)}) copy-start(f32[32]{0:T(128)} %param.8) | copy-start | bytes 388
  2.2 10.0 %all-to-all-start = ((f32[128,4,32]{0,2,1:T(8,128)}), f32[128,4,32]{0,2,1:T(8,128)S(1)}, u32[]{:S(2)}, u32[]{:S(2)}) async-start(f32[128,4,32]{0,2,1:T(8,128)} %bitcast), calls=%async_computation | async-start | bytes 131072 | tf_op jit(solution)/shard_map/all_to_all | solution.py:17
  12.3 28.8 %all-to-all-start.1 = ((bf16[32,128,128]{1,0,2:T(8,128)(2,1)}), bf16[32,128,128]{1,0,2:T(8,128)(2,1)S(1)}, u32[]{:S(2)}, u32[]{:S(2)}) async-start(bf16[32,128,128]{1,0,2:T(8,128)(2,1)} %copy.40), calls=%async_computation.1 | async-start | bytes 2097152 | tf_op jit(solution)/shard_map/all_to_all | solution.py:16
  47.5 3.7 %copy-start = (f32[8]{0:T(128)S(1)}, f32[8]{0:T(128)}, u32[]{:S(2)}) copy-start(f32[8]{0:T(128)} %param.9) | copy-start | bytes 100
